TPU v7x, 32 devices: a whole 2x2x4 slice. The times are simulated.
32 devices in a mesh: fsdp: 8 (over z, y), tensor: 4 (over x, core).
Axes of the slice: x: 2, y: 2, z: 4, core: 2. Of those that a mesh axis runs over, the one named last changes fastest.
Arguments:
- activations: bfloat16 [8192, 5120], P('fsdp', 'tensor'), may hold values from -6 to 6
- cotangent: bfloat16 [8192, 5120], P('fsdp', 'tensor'), may hold values from -0.06591797 to 0.06591797
- weights: float32 [5120, 5120], P(None, ('tensor', 'fsdp')), may hold values from -0.025 to 0.025
- first_moment: float32 [5120, 5120], P(None, ('tensor', 'fsdp')), may hold values from -3 to 3
- second_moment: float32 [5120, 5120], P(None, ('tensor', 'fsdp')), may hold values from 0.01 to 1
Outputs:
- weights_new: float32 [5120, 5120], P('fsdp', 'tensor')
- first_new: float32 [5120, 5120], P('fsdp', 'tensor')
- second_new: float32 [5120, 5120], P('fsdp', 'tensor')
- weights_bf16: bfloat16 [5120, 5120], P(None, 'tensor')
All inputs are finite; a program needn't handle non-finite values.
Results may differ from a plain program's by a relative error of at most 0.014.
Values may be sent and summed in bfloat16 or wider, within the bound.
A program may use at most 128 MiB of HBM per device.

v0:
```python
import jax
import jax.numpy as jnp
from jax import lax
from jax.sharding import PartitionSpec as P

STEP = 20


beta_one = 0.9
beta_two = 0.95
adam_eps = 1e-08
learn_rate = 0.0003
decay_rate = 0.1


def adam_update(weights, first_moment, second_moment, gradient):
    first_new = beta_one * first_moment + (1.0 - beta_one) * gradient
    second_new = beta_two * second_moment + (1.0 - beta_two) * gradient * gradient
    corrected = first_new / (1.0 - beta_one**STEP)
    scaled = jnp.sqrt(second_new / (1.0 - beta_two**STEP)) + adam_eps
    weights_new = weights - learn_rate * (corrected / scaled + decay_rate * weights)
    return (weights_new, first_new, second_new)


def body(activations, cotangent, weights, first_moment, second_moment):
    gathered = lax.all_gather(activations, "tensor", axis=1, tiled=True)
    transposed = lax.psum_scatter(
        lax.dot_general(
            cotangent, gathered, (((0,), (0,)), ((), ())), preferred_element_type=jnp.float32
        ).astype(jnp.bfloat16),
        "fsdp",
        scatter_dimension=0,
        tiled=True,
    ).astype(jnp.float32)
    gradient = transposed.T
    weights_old, first_old, second_old = adam_update(weights, first_moment, second_moment, gradient)
    weights_bf16 = lax.all_gather(weights_old.astype(jnp.bfloat16), "fsdp", axis=1, tiled=True)
    weights_new, first_new, second_new = (
        lax.all_to_all(
            weights_old.astype(jnp.bfloat16), "fsdp", split_axis=0, concat_axis=1, tiled=True
        ).astype(weights_old.dtype),
        lax.all_to_all(
            first_old.astype(jnp.bfloat16), "fsdp", split_axis=0, concat_axis=1, tiled=True
        ).astype(first_old.dtype),
        lax.all_to_all(
            second_old.astype(jnp.bfloat16), "fsdp", split_axis=0, concat_axis=1, tiled=True
        ).astype(second_old.dtype),
    )
    return (weights_new, first_new, second_new, weights_bf16)


def solution(mesh):
    return jax.shard_map(
        body,
        mesh=mesh,
        in_specs=(
            P("fsdp", "tensor"),
            P("fsdp", "tensor"),
            P(None, ("tensor", "fsdp")),
            P(None, ("tensor", "fsdp")),
            P(None, ("tensor", "fsdp")),
        ),
        out_specs=(
            P("fsdp", "tensor"),
            P("fsdp", "tensor"),
            P("fsdp", "tensor"),
            P(None, "tensor"),
        ),
        check_vma=False,
    )
```

profile of v0, /device:TPU:0, one launch (start us, length us, event | category | flops | bytes accessed | tf_op | source)
XLA Modules:
  0.0 621.7 jit_solution(10399196244834820)
XLA Ops:
  7.2 0.0 copy-start
  7.2 0.0 all-gather.3.cloned.1.call-start
  7.2 0.7 all-gather.3.cloned.1.call-update
  7.9 0.0 reduce-scatter.2.cloned.1.call-start
  8.0 74.5 %all-gather.3.cloned.1.call-done = bf16[1024,5120]{1,0:T(8,128)(2,1)} async-done(((bf16[1024,1280]{1,0:T(8,128)(2,1)}), bf16[1024,5120]{1,0:T(8,128)(2,1)}) %all-gather.3.cloned.1.call-update) | async-done | bytes 10485776 | tf_op jit(solution)/shard_map/all_gather | solution.py:26
  82.5 0.0 copy-done
  82.5 20.2 %convolution_convert_fusion = bf16[1280,5120]{1,0:T(8,128)(2,1)} fusion(bf16[1024,1280]{1,0:T(8,128)(2,1)S(1)} %copy-done, bf16[1024,5120]{1,0:T(8,128)(2,1)} %all-gather.3.cloned.1.call-done), kind=kOutput, calls=%fused_computation | convolution fusion | flops 13428326400 | bytes 26214400 | tf_op jit(solution)/shard_map/dot_general | solution.py:28
  102.7 0.0 reduce-scatter.2.cloned.1.call-update
  102.7 0.0 all-gather.5.cloned.1.call-start
  102.7 214.8 %reduce-scatter.2.cloned.1.call-done = bf16[160,5120]{1,0:T(8,128)(2,1)} async-done(((bf16[1280,5120]{1,0:T(8,128)(2,1)}), bf16[160,5120]{1,0:T(8,128)(2,1)}) %reduce-scatter.2.cloned.1.call-update) | async-done | bytes 1638416 | tf_op jit(solution)/shard_map/reduce_scatter | solution.py:27
  317.6 6.8 %fusion.3 = (bf16[5120,160]{0,1:T(8,128)(2,1)}, bf16[5120,160]{0,1:T(8,128)(2,1)}, bf16[5120,160]{0,1:T(8,128)(2,1)S(1)}) fusion(bf16[160,5120]{1,0:T(8,128)(2,1)} %reduce-scatter.2.cloned.1.call-done, f32[5120,160]{0,1:T(8,128)} %param.9, f32[5120,160]{0,1:T(8,128)} %param.7, f32[5120,160]{0,1:T(8,128)} %param.8), kind=kLoop, calls=%fused_computation.7 | loop fusion | flops 15564800 | bytes 16384000 | tf_op jit(solution)/shard_map/convert_element_type | solution.py:46
  324.4 0.0 all-gather.5.cloned.1.call-update
  324.5 1.3 copy.27
  325.8 4.3 all-to-all-start.1
  330.1 0.0 copy-start.2
  330.1 3.1 copy.26
  333.2 74.4 %all-to-all-done.1 = bf16[8,640,160]{1,2,0:T(8,128)(2,1)} async-done(((bf16[8,640,160]{1,2,0:T(8,128)(2,1)}), bf16[8,640,160]{1,2,0:T(8,128)(2,1)}, u32[]{:S(2)}, u32[]{:S(2)}) %all-to-all-start.1) | async-done | bytes 1638432 | tf_op jit(solution)/shard_map/all_to_all | solution.py:42
  407.7 7.6 %all-to-all-start.2 = ((bf16[8,640,160]{1,2,0:T(8,128)(2,1)}), bf16[8,640,160]{1,2,0:T(8,128)(2,1)}, u32[]{:S(2)}, u32[]{:S(2)}) async-start(bf16[8,640,160]{1,2,0:T(8,128)(2,1)} %bitcast.41), calls=%async_computation.3 | async-start | bytes 3276800 | tf_op jit(solution)/shard_map/all_to_all | solution.py:45
  415.3 0.0 copy-done.2
  415.3 1.3 copy.28
  416.6 78.4 %all-to-all-done.2 = bf16[8,640,160]{1,2,0:T(8,128)(2,1)} async-done(((bf16[8,640,160]{1,2,0:T(8,128)(2,1)}), bf16[8,640,160]{1,2,0:T(8,128)(2,1)}, u32[]{:S(2)}, u32[]{:S(2)}) %all-to-all-start.2) | async-done | bytes 1638432 | tf_op jit(solution)/shard_map/all_to_all | solution.py:45
  495.0 3.6 all-to-all-start
  498.6 3.4 convert_element_type.59
  502.0 4.6 copy.18
  506.5 3.4 convert_element_type.58
  509.9 4.6 copy.17
  514.4 59.6 %all-to-all-done = bf16[8,640,160]{1,2,0:T(8,128)(2,1)S(1)} async-done(((bf16[8,640,160]{1,2,0:T(8,128)(2,1)}), bf16[8,640,160]{1,2,0:T(8,128)(2,1)S(1)}, u32[]{:S(2)}, u32[]{:S(2)}) %all-to-all-start) | async-done | bytes 1638432 | tf_op jit(solution)/shard_map/all_to_all | solution.py:39
  574.0 1.9 convert_element_type.57
  576.0 4.6 copy.16
  580.5 17.0 %all-gather.5.cloned.1.call-done = bf16[5120,1280]{0,1:T(8,128)(2,1)} async-done(((bf16[5120,160]{0,1:T(8,128)(2,1)}), bf16[5120,1280]{0,1:T(8,128)(2,1)}) %all-gather.5.cloned.1.call-update) | async-done | bytes 13107216 | tf_op jit(solution)/shard_map/all_gather | solution.py:37
  597.5 0.0 copy-start.1
  597.5 17.7 %copy.19 = bf16[5120,1280]{1,0:T(8,128)(2,1)} copy(bf16[5120,1280]{0,1:T(8,128)(2,1)} %all-gather.5.cloned.1.call-done) | data formatting | bytes 26214400
  615.2 0.0 copy-done.1
Async XLA Ops:
  7.2 75.3 %copy-start = (bf16[1024,1280]{1,0:T(8,128)(2,1)S(1)}, bf16[1024,1280]{1,0:T(8,128)(2,1)}, u32[]{:S(2)}) copy-start(bf16[1024,1280]{1,0:T(8,128)(2,1)} %param.6) | copy-start | bytes 7864324
  7.2 75.3 %all-gather.3.cloned.1.call-start = ((), (), s32[]{:S(2)}) async-start(), calls=%async_computation.4 | async-start | bytes 13107200 | tf_op jit(solution)/shard_map/all_gather | solution.py:26
  7.9 309.7 %reduce-scatter.2.cloned.1.call-start = ((), (), s32[]{:S(2)}) async-start(), calls=%async_computation.5 | async-start | bytes 14745600 | tf_op jit(solution)/shard_map/reduce_scatter | solution.py:27
  102.7 494.8 %all-gather.5.cloned.1.call-start = ((), (), s32[]{:S(2)}) async-start(), calls=%async_computation.6 | async-start | bytes 14745600 | tf_op jit(solution)/shard_map/all_gather | solution.py:37
  325.8 81.9 %all-to-all-start.1 = ((bf16[8,640,160]{1,2,0:T(8,128)(2,1)}), bf16[8,640,160]{1,2,0:T(8,128)(2,1)}, u32[]{:S(2)}, u32[]{:S(2)}) async-start(bf16[8,640,160]{1,2,0:T(8,128)(2,1)} %bitcast.34), calls=%async_computation.2 | async-start | bytes 3276800 | tf_op jit(solution)/shard_map/all_to_all | solution.py:42
  330.1 85.2 %copy-start.2 = (bf16[5120,160]{0,1:T(8,128)(2,1)S(1)}, bf16[5120,160]{0,1:T(8,128)(2,1)}, u32[]{:S(2)}) copy-start(bf16[5120,160]{0,1:T(8,128)(2,1)} %get-tuple-element.13) | copy-start | bytes 4915204
  407.7 87.3 %all-to-all-start.2 = ((bf16[8,640,160]{1,2,0:T(8,128)(2,1)}), bf16[8,640,160]{1,2,0:T(8,128)(2,1)}, u32[]{:S(2)}, u32[]{:S(2)}) async-start(bf16[8,640,160]{1,2,0:T(8,128)(2,1)} %bitcast.41), calls=%async_computation.3 | async-start | bytes 3276800 | tf_op jit(solution)/shard_map/all_to_all | solution.py:45
  495.0 79.0 %all-to-all-start = ((bf16[8,640,160]{1,2,0:T(8,128)(2,1)}), bf16[8,640,160]{1,2,0:T(8,128)(2,1)S(1)}, u32[]{:S(2)}, u32[]{:S(2)}) async-start(bf16[8,640,160]{1,2,0:T(8,128)(2,1)} %bitcast.40), calls=%async_computation.1 | async-start | bytes 3276800 | tf_op jit(solution)/shard_map/all_to_all | solution.py:39
  597.5 17.7 %copy-start.1 = (bf16[1024,1280]{1,0:T(8,128)(2,1)S(1)}, bf16[1024,1280]{1,0:T(8,128)(2,1)}, u32[]{:S(2)}) copy-start(bf16[1024,1280]{1,0:T(8,128)(2,1)} %param.6) | copy-start | bytes 7864324
Sparse Core Ops, SparseCore 0:
  9.6 72.8 all-gather.2
  102.8 214.7 reduce-scatter.1
  324.6 272.8 all-gather.4
where the time goes:
time: 623 us; the launch traced here: 622 us
  waiting for transfers between devices  519 us (83%)
  local copies, waits for them, and re-layouts  37.1 us (6%)
  matrix products  20.2 us (3%)
  starting transfers between devices  15.7 us (3%)
  other arithmetic  15.5 us (2%)
  between operations  13.8 us (2%)
    reduce_scatter x1, waiting for transfers between devices, body(): lax.psum_scatter(lax.dot_general(cotangent, gathered, (((0,), (0,)), ((),...  215 us
    all_to_all x1, waiting for transfers between devices, body(): lax.all_to_all(second_old.astype(jnp.bfloat16), 'fsdp', split_axis=0, con...  78.4 us
    all_gather x1, waiting for transfers between devices, body(): gathered = lax.all_gather(activations, 'tensor', axis=1, tiled=True)  74.5 us
    all_to_all x1, waiting for transfers between devices, body(): lax.all_to_all(first_old.astype(jnp.bfloat16), 'fsdp', split_axis=0, conc...  74.4 us
    all_to_all x1, waiting for transfers between devices, body(): lax.all_to_all(weights_old.astype(jnp.bfloat16), 'fsdp', split_axis=0, co...  59.6 us
    unnamed x10, local copies, waits for them, and re-layouts  31.4 us
    dot_general x1, matrix products, body(): lax.dot_general(cotangent, gathered, (((0,), (0,)), ((), ())), preferred_...  20.2 us
    all_gather x1, waiting for transfers between devices, body(): lax.all_gather(weights_old.astype(jnp.bfloat16), 'fsdp', axis=1, tiled=True)  17 us
  transfers between devices with their start and end apart: 6, of which 6 were waited for; matrix products, arithmetic and copies ran while one was open for 5% of the time, Pallas kernels for 0%

commit v1 on v0

v1 whole, which is shorter than its diff:
```python
import functools

import jax
import jax.numpy as jnp
from jax import lax
from jax.experimental import pallas as pl
from jax.experimental.pallas import tpu as pltpu
from jax.sharding import PartitionSpec as P


STEP = 20


beta_one = 0.9
beta_two = 0.95
adam_eps = 1e-08
learn_rate = 0.0003
decay_rate = 0.1


def adam_update(weights, first_moment, second_moment, gradient):
    first_new = beta_one * first_moment + (1.0 - beta_one) * gradient
    second_new = beta_two * second_moment + (1.0 - beta_two) * gradient * gradient
    corrected = first_new / (1.0 - beta_one**STEP)
    scaled = jnp.sqrt(second_new / (1.0 - beta_two**STEP)) + adam_eps
    weights_new = weights - learn_rate * (corrected / scaled + decay_rate * weights)
    return (weights_new, first_new, second_new)


def line_pairs(length, step, senders):
    return [
        (2 * z + p, 2 * (z + step) + p)
        for z in range(length)
        for p in range(2)
        if senders(z) and 0 <= z + step < length
    ]


def reduce_line(term, z, length):
    last = length - 1
    right = left = None
    for s in range(last):
        up = term(jnp.clip(last + z - s, 0, last))
        down = term(jnp.clip(s - last + z, 0, last))
        if s:
            up = (up.astype(jnp.float32) + right.astype(jnp.float32)).astype(jnp.bfloat16)
            down = (down.astype(jnp.float32) + left.astype(jnp.float32)).astype(jnp.bfloat16)
        right = lax.ppermute(up, "fsdp", line_pairs(length, 1, lambda i: i <= s))
        left = lax.ppermute(down, "fsdp", line_pairs(length, -1, lambda i: i >= last - s))
    own = term(z)
    own = own.astype(jnp.float32)
    if last:
        own = own + right.astype(jnp.float32) + left.astype(jnp.float32)
    return own


def gather_kernel(
    length, own_ref, out_ref, local_sem, y_send, y_recv, r_send, r_recv, l_send, l_recv
):
    f = lax.axis_index("fsdp")
    z, p = f // 2, f % 2
    last = length - 1
    rows = own_ref.shape[0]
    pair, right, left = f + 1 - 2 * p, f + 2, f - 2

    def block(c):
        return out_ref.at[pl.ds((2 * c + p) * rows, rows)]

    def copy(src, dst, send, recv, target):
        return pltpu.make_async_remote_copy(
            src_ref=src,
            dst_ref=dst,
            send_sem=send,
            recv_sem=recv,
            device_id={"fsdp": target},
            device_id_type=pl.DeviceIdType.MESH,
        )

    def to_pair(c, src=None):
        return copy(block(c) if src is None else src, block(c), y_send.at[c], y_recv.at[c], pair)

    def to_right(s, src=None):
        c = z - s
        return copy(block(c) if src is None else src, block(c), r_send.at[s], r_recv.at[s], right)

    def to_left(s, src=None):
        c = z + s
        return copy(block(c) if src is None else src, block(c), l_send.at[s], l_recv.at[s], left)

    barrier = pltpu.get_barrier_semaphore()
    pl.semaphore_signal(
        barrier, inc=1, device_id={"fsdp": pair}, device_id_type=pl.DeviceIdType.MESH
    )

    @pl.when(z > 0)
    def _():
        pl.semaphore_signal(
            barrier, inc=1, device_id={"fsdp": left}, device_id_type=pl.DeviceIdType.MESH
        )

    @pl.when(z < last)
    def _():
        pl.semaphore_signal(
            barrier, inc=1, device_id={"fsdp": right}, device_id_type=pl.DeviceIdType.MESH
        )

    span = max(last, 1)
    pl.semaphore_wait(barrier, 1 + (z + span - 1) // span + (last - z + span - 1) // span)

    @pl.when(z < last)
    def _():
        to_right(0, own_ref).start()

    @pl.when(z > 0)
    def _():
        to_left(0, own_ref).start()

    to_pair(z, own_ref).start()
    here = pltpu.make_async_copy(own_ref, block(z), local_sem)
    here.start()

    for s in range(last):

        @pl.when(z > s)
        def _():
            c = z - 1 - s
            copy(block(c), block(c), r_send.at[s], r_recv.at[s], left).wait_recv()
            if s + 1 < last:

                @pl.when(z < last)
                def _():
                    to_right(s + 1).start()

            to_pair(c).start()

        @pl.when(z < last - s)
        def _():
            c = z + 1 + s
            copy(block(c), block(c), l_send.at[s], l_recv.at[s], right).wait_recv()
            if s + 1 < last:

                @pl.when(z > 0)
                def _():
                    to_left(s + 1).start()

            to_pair(c).start()

    for s in range(last):

        @pl.when((z < last) & (z >= s))
        def _():
            to_right(s).wait_send()

        @pl.when((z > 0) & (last - z >= s))
        def _():
            to_left(s).wait_send()

    here.wait()
    for c in range(length):
        to_pair(c).wait_send()
        theirs = out_ref.at[pl.ds((2 * c + 1 - p) * rows, rows)]
        copy(theirs, theirs, y_send.at[c], y_recv.at[c], pair).wait_recv()


def gather_line(own, length):
    rows, cols = own.shape
    dma = pltpu.SemaphoreType.DMA
    steps = max(length - 1, 1)
    return pl.pallas_call(
        functools.partial(gather_kernel, length),
        out_shape=jax.ShapeDtypeStruct((2 * length * rows, cols), own.dtype),
        in_specs=[pl.BlockSpec(memory_space=pltpu.VMEM)],
        out_specs=pl.BlockSpec(memory_space=pl.ANY),
        scratch_shapes=[dma, dma((length,)), dma((length,))] + [dma((steps,))] * 4,
        compiler_params=pltpu.CompilerParams(collective_id=0, has_side_effects=True),
        name="gather_rows",
    )(own)


def body(activations, cotangent, weights, first_moment, second_moment, *, n, parts):
    f = lax.axis_index("fsdp")
    z, p = f // 2, f % 2
    length = n // 2
    depth, cols = weights.shape
    rows = depth // n
    tok, width = activations.shape
    pair = [(i, i ^ 1) for i in range(n)]

    packed = jnp.concatenate([weights, first_moment, second_moment], axis=1).astype(jnp.bfloat16)
    lines = [[2 * i + q for i in range(length)] for q in range(2)]
    packed = lax.optimization_barrier(packed.reshape(length, 2, rows, 3 * cols))
    along = lax.all_to_all(packed, "fsdp", 0, 0, axis_index_groups=lines)
    blocks = activations.reshape(tok, width // (2 * rows), 2, rows)
    keep = lax.dynamic_index_in_dim(blocks, p, 2, False).reshape(tok, width // 2)
    give = lax.dynamic_index_in_dim(blocks, 1 - p, 2, False).reshape(tok, width // 2)
    got = lax.ppermute(give, "fsdp", pair)
    cot_peer = lax.ppermute(cotangent, "fsdp", pair)
    mine = lax.all_gather(keep, "tensor")
    theirs = lax.all_gather(got, "tensor")

    def product(a, b):
        return lax.dot_general(a, b, (((0,), (0,)), ((), ())), preferred_element_type=jnp.float32)

    groups = length // parts

    def term(c):
        at = (c // groups, 0, (c % groups) * rows)
        near, far = (
            lax.dynamic_slice(array, at, (1, tok, rows))[0] for array in (mine, theirs)
        )
        total = product(near, cotangent) + product(far, cot_peer)
        return lax.optimization_barrier(total.astype(jnp.bfloat16))

    gradient = reduce_line(term, z, length)

    stay = lax.dynamic_index_in_dim(along, p, 1, False)
    across = lax.ppermute(lax.dynamic_index_in_dim(along, 1 - p, 1, False), "fsdp", pair)
    moved = jnp.where(p == 0, jnp.stack([stay, across], 1), jnp.stack([across, stay], 1))

    def owned(k):
        pieces = [moved[i // 2, i % 2, :, k * cols : (k + 1) * cols] for i in range(n)]
        return lax.optimization_barrier(jnp.concatenate(pieces, axis=1)).astype(jnp.float32)

    weights_new, first_new, second_new = adam_update(owned(0), owned(1), owned(2), gradient)
    rounded = weights_new.astype(jnp.bfloat16)
    weights_bf16 = gather_line(rounded, length)
    return (weights_new, first_new, second_new, weights_bf16)


def solution(mesh):
    n, parts = mesh.shape["fsdp"], mesh.shape["tensor"]

    def run(*arrays):
        return body(*arrays, n=n, parts=parts)

    return jax.shard_map(
        run,
        mesh=mesh,
        in_specs=(
            P("fsdp", "tensor"),
            P("fsdp", "tensor"),
            P(None, ("tensor", "fsdp")),
            P(None, ("tensor", "fsdp")),
            P(None, ("tensor", "fsdp")),
        ),
        out_specs=(
            P("fsdp", "tensor"),
            P("fsdp", "tensor"),
            P("fsdp", "tensor"),
            P(None, "tensor"),
        ),
        check_vma=False,
    )
```

time: 623 us -> 503 us (0.81); the launches traced: 622 us -> 495 us
  waiting for transfers between devices: 519 us -> 151 us
  Pallas kernels: 0 us -> 142 us
  matrix products: 20.2 us -> 55.7 us
  local copies, waits for them, and re-layouts: 37.1 us -> 72.2 us
  other arithmetic: 15.5 us -> 32.2 us
  starting transfers between devices: 15.7 us -> 26.9 us
    reduce_scatter x1 -> x0, waiting for transfers between devices: 215 us -> none  [body(): lax.psum_scatter(lax.dot_general(cotangent, gathered, (((0,), (0,)), ((),...]
    pallas_call x0 -> x1, Pallas kernels: none -> 142 us  [gather_line(): pl.pallas_call(functools.partial(gather_kernel, length), out_shape=jax.Sh...]
    all_to_all x3 -> x1, waiting for transfers between devices: 212 us -> 73.7 us  [body(): along = lax.all_to_all(packed, 'fsdp', 0, 0, axis_index_groups=lines)]
    all_gather x2, waiting for transfers between devices: 91.5 us -> 0.01 us  [the longest x1 0.01 us: body(): mine = lax.all_gather(keep, 'tensor')]
    ppermute x0 -> x9, waiting for transfers between devices: none -> 77.5 us  [the longest x3 48.2 us: reduce_line(): right = lax.ppermute(up, 'fsdp', line_pairs(length, 1, lambda i: i <= s))]
    dot_general x1 -> x14, matrix products: 20.2 us -> 55.7 us  [product(): lax.dot_general(a, b, (((0,), (0,)), ((), ())), preferred_element_type=jn...]
    concatenate x0 -> x6, local copies, waits for them, and re-layouts: none -> 22.8 us  [the longest x3 12.3 us: owned(): jnp.concatenate(pieces, axis=1)]
    ppermute x0 -> x9, starting transfers between devices: none -> 20.7 us  [the longest x3 12.2 us: reduce_line(): right = lax.ppermute(up, 'fsdp', line_pairs(length, 1, lambda i: i <= s))]
  transfers between devices with their start and end apart: 6 -> 12, of which waited for: 6 -> 5; matrix products, arithmetic and copies ran while one was open for 5% -> 28% of each run, Pallas kernels for 0% -> 0%
where the time goes in v1:
time: 503 us; the launch traced here: 495 us
  waiting for transfers between devices  151 us (30%)
  Pallas kernels  142 us (28%)
  local copies, waits for them, and re-layouts  72.2 us (14%)
  matrix products  55.7 us (11%)
  other arithmetic  32.2 us (6%)
  starting transfers between devices  26.9 us (5%)
  between operations  14.8 us (3%)
    pallas_call x1, Pallas kernels, gather_line(): pl.pallas_call(functools.partial(gather_kernel, length), out_shape=jax.Sh...  142 us
    all_to_all x1, waiting for transfers between devices, body(): along = lax.all_to_all(packed, 'fsdp', 0, 0, axis_index_groups=lines)  73.7 us
    dot_general x14, matrix products, product(): lax.dot_general(a, b, (((0,), (0,)), ((), ())), preferred_element_type=jn...  55.7 us
    ppermute x3, waiting for transfers between devices, reduce_line(): right = lax.ppermute(up, 'fsdp', line_pairs(length, 1, lambda i: i <= s))  48.2 us
    ppermute x1, waiting for transfers between devices, body(): got = lax.ppermute(give, 'fsdp', pair)  29.3 us
    unnamed x23, local copies, waits for them, and re-layouts  18.2 us
    concatenate x3, local copies, waits for them, and re-layouts, owned(): jnp.concatenate(pieces, axis=1)  12.3 us
    ppermute x3, starting transfers between devices, reduce_line(): right = lax.ppermute(up, 'fsdp', line_pairs(length, 1, lambda i: i <= s))  12.2 us
  transfers between devices with their start and end apart: 12, of which 5 were waited for; matrix products, arithmetic and copies ran while one was open for 28% of the time, Pallas kernels for 0%

profile of v1, /device:TPU:0, one launch (start us, length us, event | category | flops | bytes accessed | tf_op | source)
XLA Modules:
  0.0 495.0 jit_solution(7506326668886165322)
XLA Ops:
  7.2 0.0 all-gather.5.cloned.1.call-start
  7.2 3.0 copy.29
  10.2 1.7 constant_dynamic-slice_fusion
  12.0 0.0 all-gather.5.cloned.1.call-update
  12.0 2.1 convert.12
  14.1 1.3 concatenate.20
  15.4 3.3 convert.13
  18.7 4.2 concatenate.21
  22.9 3.9 convert.14
  26.8 5.1 %concatenate.22 = bf16[4,2,640,160]{2,1,0,3:T(2,128)(2,1)} reshape(bf16[5120,160]{0,1:T(8,128)(2,1)} %convert.14) | data formatting | bytes 3276800 | tf_op jit(solution)/shard_map/concatenate | solution.py:189
  31.9 8.0 %pad_maximum_fusion = bf16[4,2,640,480]{2,1,0,3:T(2,128)(2,1)S(1)} fusion(bf16[4,2,640,160]{2,1,0,3:T(2,128)(2,1)} %concatenate.22, bf16[4,2,640,160]{2,1,0,3:T(2,128)(2,1)S(1)} %concatenate.21, bf16[4,2,640,160]{2,1,0,3:T(2,128)(2,1)S(1)} %concatenate.20), kind=kLoop, calls=%fused_computation.1 | loop fusion | flops 4915200 | bytes 9830400 | tf_op jit(solution)/shard_map/concatenate | solution.py:189
  39.8 2.9 copy.26
  42.7 6.1 %all-to-all-start = ((bf16[4,2,640,480]{2,3,1,0:T(8,128)(2,1)}), bf16[4,2,640,480]{2,3,1,0:T(8,128)(2,1)}, u32[]{:S(2)}, u32[]{:S(2)}) async-start(bf16[4,2,640,480]{2,3,1,0:T(8,128)(2,1)} %copy.26), calls=%async_computation | async-start | bytes 9830400 | tf_op jit(solution)/shard_map/all_to_all | solution.py:192
  48.8 2.6 copy.31
  51.4 1.7 collective-permute-start.1
  53.1 29.3 %collective-permute-done.1 = bf16[1024,640]{1,0:T(8,128)(2,1)} collective-permute-done((bf16[1024,640]{1,0:T(8,128)(2,1)}, bf16[1024,640]{1,0:T(8,128)(2,1)}, u32[]{:S(2)}, u32[]{:S(2)}) %collective-permute-start.1) | collective-permute-done | bytes 1310752 | tf_op jit(solution)/shard_map/ppermute | solution.py:196
  82.4 0.0 all-gather.7.cloned.1.call-update
  82.4 1.8 collective-permute-start.2
  84.3 73.7 %all-to-all-done = bf16[4,2,640,480]{2,3,1,0:T(8,128)(2,1)} async-done(((bf16[4,2,640,480]{2,3,1,0:T(8,128)(2,1)}), bf16[4,2,640,480]{2,3,1,0:T(8,128)(2,1)}, u32[]{:S(2)}, u32[]{:S(2)}) %all-to-all-start) | async-done | bytes 4915232 | tf_op jit(solution)/shard_map/all_to_all | solution.py:192
  157.9 5.1 %constant_dynamic-slice_fusion.2 = (bf16[4,1,640,480]{2,3,1,0:T(8,128)(2,1)}, bf16[4,640,480]{1,2,0:T(8,128)(2,1)}) fusion(bf16[4,2,640,480]{2,3,1,0:T(8,128)(2,1)} %all-to-all-done, s32[]{:T(128)S(6)} %select_n.82, s32[]{:T(128)S(6)} %select_n.83), kind=kLoop, calls=%fused_computation.104 | loop fusion | bytes 9830408 | tf_op jit(solution)/shard_map/jit(dynamic_index_in_dim)/dynamic_slice | solution.py:216
  163.0 4.4 copy.32
  167.4 1.7 collective-permute-start
  169.1 8.3 %copy.30 = bf16[4096,1,1,640]{3,0,2,1:T(8,128)(2,1)} copy(bf16[4096,1,1,640]{0,3,2,1:T(8,128)(2,1)} %all-gather.5.cloned.1.call-done) | data formatting | bytes 10485760 | tf_op jit(solution)/shard_map/all_gather | solution.py:198
  177.4 0.0 copy-start.1
  177.4 5.1 %fusion.11 = f32[640,1280]{1,0:T(8,128)} fusion(bf16[1024,1280]{1,0:T(8,128)(2,1)S(1)} %copy-done, bf16[4,1024,640]{2,1,0:T(8,128)(2,1)} %bitcast.117, s32[]{:T(128)S(6)} %min.24), kind=kOutput, calls=%fused_computation.30 | convolution fusion | flops 1677721600 | bytes 7208964 | tf_op jit(solution)/shard_map/dot_general | solution.py:202
  182.5 3.6 fusion.14
  186.1 3.6 fusion.17
  189.7 3.6 fusion.20
  193.3 3.6 fusion.23
  196.9 3.6 fusion.26
  200.5 3.7 fusion.29
  204.4 0.0 copy-start.8
  204.4 5.2 %fusion.9 = bf16[640,1280]{1,0:T(8,128)(2,1)S(1)} fusion(f32[640,1280]{1,0:T(8,128)} %fusion.11, bf16[1024,1280]{1,0:T(8,128)(2,1)} %collective-permute-done.2, bf16[4,1024,640]{2,1,0:T(8,128)(2,1)} %bitcast.127, s32[]{:T(128)S(6)} %min.24), kind=kOutput, calls=%fused_computation.27 | convolution fusion | flops 1679360000 | bytes 8847364 | tf_op jit(solution)/shard_map/dot_general | solution.py:202
  209.6 0.0 copy-start.6
  209.6 0.9 collective-permute-start.6
  210.5 3.8 fusion.6
  214.3 1.7 collective-permute-start.3
  215.9 3.8 fusion.8
  219.7 3.8 fusion.5
  223.5 0.4 add_convert_fusion.1
  223.9 0.0 copy-start.4
  223.9 0.9 collective-permute-start.7
  224.8 25.4 %collective-permute-done.3 = bf16[640,1280]{1,0:T(8,128)(2,1)S(1)} collective-permute-done((bf16[640,1280]{1,0:T(8,128)(2,1)S(1)}, bf16[640,1280]{1,0:T(8,128)(2,1)S(1)}, u32[]{:S(2)}, u32[]{:S(2)}) %collective-permute-start.3) | collective-permute-done | bytes 1638432 | tf_op jit(solution)/shard_map/ppermute | solution.py:48
  250.2 0.4 add_convert_fusion.3
  250.7 5.0 %collective-permute-start.4 = (bf16[640,1280]{1,0:T(8,128)(2,1)S(1)}, bf16[640,1280]{1,0:T(8,128)(2,1)S(1)}, u32[]{:S(2)}, u32[]{:S(2)}) collective-permute-start(bf16[640,1280]{1,0:T(8,128)(2,1)S(1)} %add_convert_fusion.3), channel_id=1, source_target_pairs={{0,8},{4,12},{8,16},{12,20},{1,9},{5,13},{9,17},{13,21},{2,10},{6,... | collective-permute-start | bytes 4915208 | tf_op jit(solution)/shard_map/ppermute | solution.py:48
  255.6 3.8 fusion.7
  259.4 3.8 fusion.4
  263.2 1.6 add_convert_fusion
  264.8 1.5 collective-permute-start.8
  266.3 22.6 %collective-permute-done.4 = bf16[640,1280]{1,0:T(8,128)(2,1)S(1)} collective-permute-done((bf16[640,1280]{1,0:T(8,128)(2,1)S(1)}, bf16[640,1280]{1,0:T(8,128)(2,1)S(1)}, u32[]{:S(2)}, u32[]{:S(2)}) %collective-permute-start.4) | collective-permute-done | bytes 1638432 | tf_op jit(solution)/shard_map/ppermute | solution.py:48
  288.9 1.6 add_convert_fusion.2
  290.4 5.5 %collective-permute-start.5 = (bf16[640,1280]{1,0:T(8,128)(2,1)}, bf16[640,1280]{1,0:T(8,128)(2,1)}, u32[]{:S(2)}, u32[]{:S(2)}) collective-permute-start(bf16[640,1280]{1,0:T(8,128)(2,1)} %add_convert_fusion.2), channel_id=1, source_target_pairs={{0,8},{4,12},{8,16},{12,20},{16,24},{20,28},{1,9},{5,13},{9,17},{1... | collective-permute-start | bytes 4915208 | tf_op jit(solution)/shard_map/ppermute | solution.py:48
  296.0 4.9 fusion.3
  300.9 4.5 copy.28
  305.4 3.8 maximum_select_fusion
  309.2 0.9 slice_bitcast_fusion.19
  310.2 5.2 %slice_bitcast_fusion = (bf16[640,160]{1,0:T(8,128)(2,1)}, bf16[640,160]{1,0:T(8,128)(2,1)}, bf16[640,160]{1,0:T(8,128)(2,1)}, bf16[640,160]{1,0:T(8,128)(2,1)},...) fusion(bf16[4,2,640,480]{3,2,1,0:T(8,128)(2,1)S(1)} %maximum_se, ...), kind=kLoop, calls=%fused_computation.64 | loop fusion | bytes 7782400 | tf_op jit(solution)/shard_map/squeeze | solution.py:221
  315.4 3.4 concatenate.24
  318.8 3.9 concatenate.26
  322.7 4.9 concatenate.25
  327.6 0.2 collective-permute-done.5
  327.8 7.2 %fusion.59 = (bf16[640,1280]{1,0:T(8,128)(2,1)}, f32[640,1280]{1,0:T(8,128)}, f32[640,1280]{1,0:T(8,128)}, f32[640,1280]{1,0:T(8,128)}) fusion(bf16[640,1280]{1,0:T(8,128)(2,1)S(1)} %concatenate.24, bf16[640,1280]{1,0:T(8,128)(2,1)} %collective-permute-done.8, bf16[640,1280]{1,0:T(8,128)(2,1)} %collective-permute-done.5, bf16[640,1280]{1,0:T(8,128)(2,1)} %fusion.3, ...), kind=kLoop, calls=%fused_computation.105 | loop fusion | flops 19660800 | bytes 21299200 | tf_op jit(solution)/shard_map/convert_element_type | solution.py:225
  335.1 142.0 %gather_rows.1 = bf16[5120,1280]{1,0:T(8,128)(2,1)} custom-call(bf16[640,1280]{1,0:T(8,128)(2,1)} %get-tuple-element.4.own_ref), custom_call_target="tpu_custom_call" | custom-call | tf_op jit(solution)/shard_map/gather_rows/pallas_call | solution.py:169
  477.1 10.8 %copy.34 = bf16[5120,1280]{1,0:T(8,128)(2,1)} copy(bf16[5120,1280]{1,0:T(8,128)(2,1)} %gather_rows.1) | data formatting | bytes 26214400
  (24 shorter events, 0.1 us)
Async XLA Ops:
  7.2 161.9 %all-gather.5.cloned.1.call-start = ((), (), s32[]{:S(2)}) async-start(), calls=%async_computation.1 | async-start | bytes 6553600 | tf_op jit(solution)/shard_map/all_gather | solution.py:198
  42.7 115.2 %all-to-all-start = ((bf16[4,2,640,480]{2,3,1,0:T(8,128)(2,1)}), bf16[4,2,640,480]{2,3,1,0:T(8,128)(2,1)}, u32[]{:S(2)}, u32[]{:S(2)}) async-start(bf16[4,2,640,480]{2,3,1,0:T(8,128)(2,1)} %copy.26), calls=%async_computation | async-start | bytes 9830400 | tf_op jit(solution)/shard_map/all_to_all | solution.py:192
  48.8 33.6 %copy-start = (bf16[1024,1280]{1,0:T(8,128)(2,1)S(1)}, bf16[1024,1280]{1,0:T(8,128)(2,1)}, u32[]{:S(2)}) copy-start(bf16[1024,1280]{1,0:T(8,128)(2,1)} %param.6) | copy-start | bytes 7864324
  48.8 155.4 %all-gather.7.cloned.1.call-start = ((), (), s32[]{:S(2)}) async-start(), calls=%async_computation.2 | async-start | bytes 6553600 | tf_op jit(solution)/shard_map/all_gather | solution.py:199
  51.4 31.0 %collective-permute-start.1 = (bf16[1024,640]{1,0:T(8,128)(2,1)}, bf16[1024,640]{1,0:T(8,128)(2,1)}, u32[]{:S(2)}, u32[]{:S(2)}) collective-permute-start(bf16[1024,640]{1,0:T(8,128)(2,1)} %bitcast.126), channel_id=1, source_target_pairs={{0,4},{4,0},{8,12},{12,8},{16,20},{20,16},{24,28},{28,24},{1,5},{5... | collective-permute-start | bytes 3932168 | tf_op jit(solution)/shard_map/ppermute | solution.py:196
  82.4 121.8 %collective-permute-start.2 = (bf16[1024,1280]{1,0:T(8,128)(2,1)S(1)}, bf16[1024,1280]{1,0:T(8,128)(2,1)}, u32[]{:S(2)}, u32[]{:S(2)}) collective-permute-start(bf16[1024,1280]{1,0:T(8,128)(2,1)S(1)} %copy-done), channel_id=1, source_target_pairs={{0,4},{4,0},{8,12},{12,8},{16,20},{20,16},{24,28},{28,24},{1,5},{5... | collective-permute-start | bytes 7864328 | tf_op jit(solution)/shard_map/ppermute | solution.py:197
  167.4 133.5 %collective-permute-start = (bf16[4,640,480]{1,2,0:T(8,128)(2,1)}, bf16[4,640,480]{1,2,0:T(8,128)(2,1)}, u32[]{:S(2)}, u32[]{:S(2)}) collective-permute-start(bf16[4,640,480]{1,2,0:T(8,128)(2,1)} %get-tuple-element.33), channel_id=1, source_target_pairs={{0,4},{4,0},{8,12},{12,8},{16,20},{20,16},{24,28},{28,24},{1,5},{5... | collective-permute-start | bytes 7372808 | tf_op jit(solution)/shard_map/ppermute | solution.py:217
  177.4 5.1 %copy-start.1 = (bf16[4096,1,1,640]{3,0,2,1:T(8,128)(2,1)S(1)}, bf16[4096,1,1,640]{3,0,2,1:T(8,128)(2,1)}, u32[]{:S(2)}) copy-start(bf16[4096,1,1,640]{3,0,2,1:T(8,128)(2,1)} %copy.30) | copy-start | bytes 15728644
  204.4 6.1 %copy-start.8 = (f32[640,1280]{1,0:T(8,128)S(1)}, f32[640,1280]{1,0:T(8,128)}, u32[]{:S(2)}) copy-start(f32[640,1280]{1,0:T(8,128)} %fusion.20) | copy-start | bytes 9830404
  204.4 6.1 %copy-start.9 = (bf16[4096,640]{1,0:T(8,128)(2,1)S(1)}, bf16[4096,640]{1,0:T(8,128)(2,1)}, u32[]{:S(2)}) copy-start(bf16[4096,640]{1,0:T(8,128)(2,1)} %all-gather.7.cloned.1.call-done) | copy-start | bytes 15728644
  209.6 6.4 %copy-start.6 = (f32[640,1280]{1,0:T(8,128)S(1)}, f32[640,1280]{1,0:T(8,128)}, u32[]{:S(2)}) copy-start(f32[640,1280]{1,0:T(8,128)} %fusion.14) | copy-start | bytes 9830404
  209.6 13.9 %collective-permute-start.6 = (bf16[640,1280]{1,0:T(8,128)(2,1)S(1)}, bf16[640,1280]{1,0:T(8,128)(2,1)S(1)}, u32[]{:S(2)}, u32[]{:S(2)}) collective-permute-start(bf16[640,1280]{1,0:T(8,128)(2,1)S(1)} %fusion.9), channel_id=1, source_target_pairs={{24,16},{28,20},{25,17},{29,21},{26,18},{30,22},{27,19},{31,23}} | collective-permute-start | bytes 4915208 | tf_op jit(solution)/shard_map/ppermute | solution.py:49
  214.3 5.5 %copy-start.7 = (f32[640,1280]{1,0:T(8,128)S(1)}, f32[640,1280]{1,0:T(8,128)}, u32[]{:S(2)}) copy-start(f32[640,1280]{1,0:T(8,128)} %fusion.23) | copy-start | bytes 9830404
  214.3 36.0 %collective-permute-start.3 = (bf16[640,1280]{1,0:T(8,128)(2,1)S(1)}, bf16[640,1280]{1,0:T(8,128)(2,1)S(1)}, u32[]{:S(2)}, u32[]{:S(2)}) collective-permute-start(bf16[640,1280]{1,0:T(8,128)(2,1)S(1)} %fusion.6), channel_id=1, source_target_pairs={{0,8},{4,12},{1,9},{5,13},{2,10},{6,14},{3,11},{7,15}} | collective-permute-start | bytes 4915208 | tf_op jit(solution)/shard_map/ppermute | solution.py:48
  223.9 31.7 %copy-start.4 = (f32[640,1280]{1,0:T(8,128)S(1)}, f32[640,1280]{1,0:T(8,128)}, u32[]{:S(2)}) copy-start(f32[640,1280]{1,0:T(8,128)} %fusion.17) | copy-start | bytes 9830404
  223.9 39.3 %collective-permute-start.7 = (bf16[640,1280]{1,0:T(8,128)(2,1)S(1)}, bf16[640,1280]{1,0:T(8,128)(2,1)S(1)}, u32[]{:S(2)}, u32[]{:S(2)}) collective-permute-start(bf16[640,1280]{1,0:T(8,128)(2,1)S(1)} %add_convert_fusion.1), channel_id=1, source_target_pairs={{16,8},{20,12},{24,16},{28,20},{17,9},{21,13},{25,17},{29,21},{18,... | collective-permute-start | bytes 4915208 | tf_op jit(solution)/shard_map/ppermute | solution.py:49
  250.6 8.8 %copy-start.5 = (f32[640,1280]{1,0:T(8,128)S(1)}, f32[640,1280]{1,0:T(8,128)}, u32[]{:S(2)}) copy-start(f32[640,1280]{1,0:T(8,128)} %fusion.26) | copy-start | bytes 9830404
  250.7 38.2 %collective-permute-start.4 = (bf16[640,1280]{1,0:T(8,128)(2,1)S(1)}, bf16[640,1280]{1,0:T(8,128)(2,1)S(1)}, u32[]{:S(2)}, u32[]{:S(2)}) collective-permute-start(bf16[640,1280]{1,0:T(8,128)(2,1)S(1)} %add_convert_fusion.3), channel_id=1, source_target_pairs={{0,8},{4,12},{8,16},{12,20},{1,9},{5,13},{9,17},{13,21},{2,10},{6,... | collective-permute-start | bytes 4915208 | tf_op jit(solution)/shard_map/ppermute | solution.py:48
  264.8 31.2 %copy-start.3 = (f32[640,1280]{1,0:T(8,128)S(1)}, f32[640,1280]{1,0:T(8,128)}, u32[]{:S(2)}) copy-start(f32[640,1280]{1,0:T(8,128)} %fusion.29) | copy-start | bytes 9830404
  264.8 62.9 %collective-permute-start.8 = (bf16[640,1280]{1,0:T(8,128)(2,1)}, bf16[640,1280]{1,0:T(8,128)(2,1)}, u32[]{:S(2)}, u32[]{:S(2)}) collective-permute-start(bf16[640,1280]{1,0:T(8,128)(2,1)} %add_convert_fusion), channel_id=1, source_target_pairs={{8,0},{12,4},{16,8},{20,12},{24,16},{28,20},{9,1},{13,5},{17,9},{2... | collective-permute-start | bytes 4915208 | tf_op jit(solution)/shard_map/ppermute | solution.py:49
  290.4 37.4 %collective-permute-start.5 = (bf16[640,1280]{1,0:T(8,128)(2,1)}, bf16[640,1280]{1,0:T(8,128)(2,1)}, u32[]{:S(2)}, u32[]{:S(2)}) collective-permute-start(bf16[640,1280]{1,0:T(8,128)(2,1)} %add_convert_fusion.2), channel_id=1, source_target_pairs={{0,8},{4,12},{8,16},{12,20},{16,24},{20,28},{1,9},{5,13},{9,17},{1... | collective-permute-start | bytes 4915208 | tf_op jit(solution)/shard_map/ppermute | solution.py:48
  300.9 4.5 copy-start.2
Sparse Core Ops, SparseCore 0:
  12.1 43.1 all-gather.4
  82.6 41.7 all-gather.6
